TPU v7x, 16 devices: a whole 2x2x2 slice. The times are simulated.
16 devices in a mesh: ez: 2 (over z), ey: 2 (over y), ex: 4 (over x, core).
Axes of the slice: x: 2, y: 2, z: 2, core: 2. Of those that a mesh axis runs over, the one named last changes fastest.
Arguments:
- tokens: bfloat16 [4096, 2048], P(('ez', 'ey', 'ex'))
- expert_ids: int32 [4096, 8], P(('ez', 'ey', 'ex'))
- gate_weights: float32 [4096, 8], P(('ez', 'ey', 'ex'))
- w_gate: bfloat16 [64, 2048, 1024], P(('ez', 'ey', 'ex'))
- w_up: bfloat16 [64, 2048, 1024], P(('ez', 'ey', 'ex'))
- w_down: bfloat16 [64, 1024, 2048], P(('ez', 'ey', 'ex'))
Outputs:
- output: bfloat16 [4096, 2048], P(('ez', 'ey', 'ex'))
All inputs are finite; a program needn't handle non-finite values.
Results may differ from a plain program's by a relative error of at most 0.00588.
Values are sent between devices in bfloat16 or wider.
A program may use at most 1 GiB of HBM per device.

v0:
```python
import math
import jax
import jax.numpy as jnp
from jax import lax
from jax.sharding import PartitionSpec as P


def pack_rows(chosen, gate_vals, per_expert):
    row_rank = jnp.cumsum(chosen.astype(jnp.int32), axis=0) - 1
    slot_idx = jnp.where(chosen, row_rank, per_expert)
    row_idx = jnp.broadcast_to(jnp.arange(chosen.shape[0])[:, None], chosen.shape)
    exp_idx = jnp.broadcast_to(jnp.arange(chosen.shape[1])[None, :], chosen.shape)
    pick_rows = jnp.zeros((chosen.shape[1], per_expert), jnp.int32).at[exp_idx, slot_idx].set(row_idx, mode="drop")
    pick_gates = jnp.zeros((chosen.shape[1], per_expert), jnp.float32).at[exp_idx, slot_idx].set(gate_vals, mode="drop")
    return pick_rows, pick_gates


def expert_ffn(x_pack, w_gate, w_up, w_down, pick_gates):
    gate_act = jnp.einsum("lch,lhf->lcf", x_pack, w_gate, preferred_element_type=jnp.float32)
    up_act = jnp.einsum("lch,lhf->lcf", x_pack, w_up, preferred_element_type=jnp.float32)
    hidden_act = (jax.nn.silu(gate_act) * up_act).astype(jnp.bfloat16)
    expert_out = jnp.einsum("lcf,lfh->lch", hidden_act, w_down, preferred_element_type=jnp.float32)
    return expert_out * pick_gates[:, :, None]


def solution(mesh):
    ep_axes = tuple(mesh.axis_names)
    num_devices = math.prod(mesh.shape[axis_name] for axis_name in ep_axes)
    row_spec = P(ep_axes, None)
    w_spec = P(ep_axes, None, None)

    def local_layer(tokens, expert_ids, gate_weights, w_gate, w_up, w_down):
        tok_dev, hidden = tokens.shape
        top_k = expert_ids.shape[1]
        local_experts = w_gate.shape[0]
        capacity = tok_dev * top_k // num_devices
        rows_recv = num_devices * capacity
        per_expert = rows_recv // local_experts
        dest_dev = expert_ids // local_experts
        dev_hit = jnp.any(dest_dev[:, :, None] == jnp.arange(num_devices)[None, None, :], axis=1)
        all_experts = jnp.arange(num_devices * local_experts)
        gate_dense = jnp.sum(jnp.where(expert_ids[:, :, None] == all_experts[None, None, :], gate_weights[:, :, None], 0.0), axis=1)
        gate_dense = gate_dense.reshape(tok_dev, num_devices, local_experts)
        slot_pos = jnp.cumsum(dev_hit.astype(jnp.int32), axis=0) - 1
        place_mask = dev_hit[:, :, None] & (slot_pos[:, :, None] == jnp.arange(capacity)[None, None, :])
        place_bf = place_mask.astype(jnp.bfloat16)
        send_rows = jnp.einsum("tdc,th->dch", place_bf, tokens, preferred_element_type=jnp.float32).astype(jnp.bfloat16)
        send_gates = jnp.sum(jnp.where(place_mask[:, :, :, None], gate_dense[:, :, None, :], 0.0), axis=0)
        recv_rows = lax.all_to_all(send_rows, ep_axes, 0, 0, tiled=True)
        recv_gates = lax.all_to_all(send_gates, ep_axes, 0, 0, tiled=True)
        flat_rows = recv_rows.reshape(rows_recv, hidden)
        flat_gates = recv_gates.reshape(rows_recv, local_experts)
        pick_rows, pick_gates = pack_rows(flat_gates > 0.0, flat_gates, per_expert)
        weighted = expert_ffn(flat_rows[pick_rows], w_gate, w_up, w_down, pick_gates)
        part_sum = jax.ops.segment_sum(weighted.reshape(-1, hidden), pick_rows.reshape(-1), num_segments=rows_recv)
        back_rows = part_sum.astype(jnp.bfloat16).reshape(num_devices, capacity, hidden)
        returned = lax.all_to_all(back_rows, ep_axes, 0, 0, tiled=True)
        moe_sum = jnp.einsum("tdc,dch->th", place_bf, returned, preferred_element_type=jnp.float32)
        return (tokens.astype(jnp.float32) + moe_sum).astype(jnp.bfloat16)

    return jax.shard_map(local_layer, mesh=mesh, in_specs=(row_spec, row_spec, row_spec, w_spec, w_spec, w_spec), out_specs=row_spec, check_vma=False)
```

profile of v0, /device:TPU:0, one launch (start us, length us, event | category | flops | bytes accessed | tf_op | source)
XLA Modules:
  0.0 341.8 jit_solution(17285295110675130223)
XLA Ops:
  0.0 0.7 add_select_fusion
  0.7 0.6 reduce-window.14
  1.6 0.8 select_reduce_fusion.1
  2.7 1.4 fusion.7
  4.1 0.5 copy.34
  4.6 3.6 %select_reduce_fusion = f32[16,128,4]{1,0,2:T(8,128)S(1)} fusion(f32[256,16,4]{1,2,0:T(4,128)S(1)} %copy.35, pred[256,16,128]{2,1,0:T(8,128)(4,1)S(1)} %copy.34), kind=kLoop, calls=%fused_computation.6 | loop fusion | flops 4186112 | bytes 622592 | tf_op jit(solution)/shard_map/reduce_sum | solution.py:48
  8.2 0.6 copy.36
  8.8 5.3 %all-to-all-start = ((f32[16,128,4]{1,2,0:T(4,128)}), f32[16,128,4]{1,2,0:T(4,128)S(1)}, u32[]{:S(2)}, u32[]{:S(2)}) async-start(f32[16,128,4]{1,2,0:T(4,128)} %copy.36), calls=%async_computation | async-start | bytes 65536 | tf_op jit(solution)/shard_map/all_to_all | solution.py:50
  14.1 7.1 %convolution_convert_fusion = bf16[16,128,2048]{2,1,0:T(8,128)(2,1)} fusion(bf16[256,2048]{1,0:T(8,128)(2,1)} %param.6, s32[256,16]{0,1:T(8,128)S(1)} %bitcast_bitcast_fusion.1, pred[256,16]{0,1:T(8,128)(4,1)S(1)} %fusion.9), kind=kOutput, calls=%fused_computation.9 | convolution fusion | flops 2152726528 | bytes 9457664 | tf_op jit(solution)/shard_map/tdc,th->dch/dot_general | solution.py:47
  21.3 3.9 %all-to-all-start.1 = ((bf16[16,128,2048]{2,1,0:T(8,128)(2,1)}), bf16[16,128,2048]{2,1,0:T(8,128)(2,1)}, u32[]{:S(2)}, u32[]{:S(2)}) async-start(bf16[16,128,2048]{2,1,0:T(8,128)(2,1)} %convolution_convert_fusion), calls=%async_computation.1 | async-start | bytes 16777216 | tf_op jit(solution)/shard_map/all_to_all | solution.py:49
  25.2 0.6 reshape.96
  25.9 1.2 reduce-window.16
  28.2 0.6 reshape.94
  29.2 0.6 reshape.102
  29.8 30.4 %scatter_custom_fusion.2 = f32[2048]{0:T(1024)S(1)} fusion(s32[8192]{0:T(1024)S(1)} %reshape.94, f32[8192]{0:T(1024)S(1)} %reshape.102, f32[]{:T(128)} %constant.41.clone.1), kind=kCustom, calls=%fused_computation.50 | custom fusion | bytes 8196
  60.3 30.6 %scatter_custom_fusion.1 = s32[2048]{0:T(1024)S(1)} fusion(s32[8192]{0:T(1024)S(1)} %reshape.94, s32[8192]{0:T(1024)S(1)} %reshape.96, s32[]{:T(128)} %constant.20.clone.1), kind=kCustom, calls=%fused_computation.52 | custom fusion | bytes 8196 | tf_op jit(solution)/shard_map/broadcast_in_dim;reshape | solution.py:55
  91.0 41.1 %all-to-all-done.1 = bf16[16,128,2048]{2,1,0:T(8,128)(2,1)} async-done(((bf16[16,128,2048]{2,1,0:T(8,128)(2,1)}), bf16[16,128,2048]{2,1,0:T(8,128)(2,1)}, u32[]{:S(2)}, u32[]{:S(2)}) %all-to-all-start.1) | async-done | bytes 8388640 | tf_op jit(solution)/shard_map/all_to_all | solution.py:49
  132.0 20.8 %gather_fusion = bf16[2048,2048]{1,0:T(8,128)(2,1)} fusion(bf16[2048,2048]{1,0:T(8,128)(2,1)} %bitcast.7, s32[2048]{0:T(1024)S(1)} %broadcast_clamp_fusion), kind=kCustom, calls=%fused_computation | custom fusion | bytes 16785408 | tf_op jit(solution)/shard_map/gather | solution.py:54
  152.8 16.9 %fusion.22 = f32[4,512,1024]{2,1,0:T(8,128)} fusion(bf16[4,512,2048]{2,1,0:T(8,128)(2,1)} %bitcast.66, bf16[4,2048,1024]{2,1,0:T(8,128)(2,1)} %param.9), kind=kOutput, calls=%fused_computation.55 | convolution fusion | flops 8589934592 | bytes 33554432 | tf_op jit(solution)/shard_map/lch,lhf->lcf/dot_general | solution.py:19
  169.7 28.0 %broadcast_multiply_fusion = f32[4,512,2048]{2,1,0:T(8,128)} fusion(f32[4,512]{1,0:T(4,128)S(1)} %reshape.74, bf16[4,1024,2048]{2,1,0:T(8,128)(2,1)} %param.11, f32[4,512,1024]{2,1,0:T(8,128)} %fusion.22, bf16[4,512,2048]{2,1,0:T(8,128)(2,1)} %bitcast.67, bf16[4,2048,1024]{2,1,0:T(8,128)(2,1)} %param.10), kind=kOutput, calls=%fused_computation.4 | convolution fusion | flops 17196646400 | bytes 67117056 | tf_op jit(solution)/shard_map/lcf,lfh->lch/dot_general | solution.py:22
  197.7 34.1 %scatter_custom_fusion = f32[2048,2048]{1,0:T(8,128)} fusion(s32[2048]{0:T(1024)S(1)} %scatter_custom_fusion.1, f32[2048,2048]{1,0:T(8,128)} %bitcast.71, f32[]{:T(128)} %constant.41.clone.1), kind=kCustom, calls=%fused_computation.7 | custom fusion | flops 4194304 | bytes 16777728 | tf_op jit(solution)/shard_map/scatter-add | solution.py:55
  231.7 6.5 %convert_element_type.26 = bf16[2048,2048]{1,0:T(8,128)(2,1)S(1)} convert(f32[2048,2048]{1,0:T(8,128)} %scatter_custom_fusion) | non-fusion elementwise | flops 4194304 | bytes 25165824 | tf_op jit(solution)/shard_map/convert_element_type | solution.py:56
  238.3 99.3 %all_to_all.15 = bf16[16,128,2048]{2,1,0:T(8,128)(2,1)S(1)} all-to-all(bf16[16,128,2048]{2,1,0:T(8,128)(2,1)S(1)} %bitcast.65), channel_id=1, replica_groups=mesh['ez'=2,'ey'=2,'ex'=4] {'ez','ey','ex'}, dimensions={0} | all-to-all | bytes 16777216 | tf_op jit(solution)/shard_map/all_to_all | solution.py:57
  337.6 4.1 %fusion.6 = bf16[256,2048]{1,0:T(8,128)(2,1)} fusion(bf16[16,128,2048]{2,1,0:T(8,128)(2,1)S(1)} %all_to_all.15, bf16[256,2048]{1,0:T(8,128)(2,1)S(1)} %copy-done, s32[256,16]{0,1:T(8,128)S(1)} %bitcast_bitcast_fusion.1, pred[256,16]{0,1:T(8,128)(4,1)S(1)} %fusion.9), kind=kOutput, calls=%fused_computation.14 | convolution fusion | flops 2150105088 | bytes 10506240 | tf_op jit(solution)/shard_map/tdc,dch->th/dot_general | solution.py:58
  (33 shorter events, 2.2 us)
Async XLA Ops:
  8.8 12.4 %all-to-all-start = ((f32[16,128,4]{1,2,0:T(4,128)}), f32[16,128,4]{1,2,0:T(4,128)S(1)}, u32[]{:S(2)}, u32[]{:S(2)}) async-start(f32[16,128,4]{1,2,0:T(4,128)} %copy.36), calls=%async_computation | async-start | bytes 65536 | tf_op jit(solution)/shard_map/all_to_all | solution.py:50
  21.2 6.3 %copy-start.2 = (s32[2]{0:T(128)S(1)}, s32[2]{0:T(128)}, u32[]{:S(2)}) copy-start(s32[2]{0:T(128)} %constant.48) | copy-start | bytes 28
  21.2 6.4 %copy-start.1 = (s32[2]{0:T(128)S(1)}, s32[2]{0:T(128)}, u32[]{:S(2)}) copy-start(s32[2]{0:T(128)} %constant.51) | copy-start | bytes 28
  21.3 110.8 %all-to-all-start.1 = ((bf16[16,128,2048]{2,1,0:T(8,128)(2,1)}), bf16[16,128,2048]{2,1,0:T(8,128)(2,1)}, u32[]{:S(2)}, u32[]{:S(2)}) async-start(bf16[16,128,2048]{2,1,0:T(8,128)(2,1)} %convolution_convert_fusion), calls=%async_computation.1 | async-start | bytes 16777216 | tf_op jit(solution)/shard_map/all_to_all | solution.py:49
  238.3 99.3 %copy-start = (bf16[256,2048]{1,0:T(8,128)(2,1)S(1)}, bf16[256,2048]{1,0:T(8,128)(2,1)}, u32[]{:S(2)}) copy-start(bf16[256,2048]{1,0:T(8,128)(2,1)} %param.6) | copy-start | bytes 3145732
where the time goes:
time: 342 us
  blocking collectives  99.3 us (29%)
  local copies, waits for them, and re-layouts  86.4 us (25%)
  matrix products  56.1 us (16%)
  other arithmetic  49.6 us (15%)
  waiting for transfers between devices  41.1 us (12%)
  starting transfers between devices  9.16 us (3%)
    all_to_all x1, blocking collectives, local_layer(): returned = lax.all_to_all(back_rows, ep_axes, 0, 0, tiled=True)  99.3 us
    all_to_all x1, waiting for transfers between devices, local_layer(): recv_rows = lax.all_to_all(send_rows, ep_axes, 0, 0, tiled=True)  41.1 us
    scatter-add x1, other arithmetic, local_layer(): jax.ops.segment_sum(weighted.reshape(-1, hidden), pick_rows.reshape(-1),...  34.1 us
    unnamed x11, local copies, waits for them, and re-layouts  31.5 us
    another operation x1, local copies, waits for them, and re-layouts, local_layer(): jax.ops.segment_sum(weighted.reshape(-1, hidden), pick_rows.reshape(-1),...  30.6 us
    dot_general x1, matrix products, expert_ffn(): jnp.einsum('lcf,lfh->lch', hidden_act, w_down, preferred_element_type=jnp...  28 us
    gather x1, local copies, waits for them, and re-layouts, local_layer(): flat_rows[pick_rows]  20.8 us
    dot_general x1, matrix products, expert_ffn(): jnp.einsum('lch,lhf->lcf', x_pack, w_gate, preferred_element_type=jnp.flo...  16.9 us
  transfers between devices with their start and end apart: 2, of which 1 were waited for; matrix products, arithmetic and copies ran while one was open for 21% of the time, Pallas kernels for 0%

commit v1 on v0

v1 whole, which is shorter than its diff:
```python
import math
import jax
import jax.numpy as jnp
from jax import lax
from jax.sharding import PartitionSpec as P


def solution(mesh):
    ep_axes = tuple(mesh.axis_names)
    num_devices = math.prod(mesh.shape[axis_name] for axis_name in ep_axes)
    row_spec = P(ep_axes, None)
    w_spec = P(ep_axes, None, None)

    def local_layer(tokens, expert_ids, gate_weights, w_gate, w_up, w_down):
        tok_dev, hidden = tokens.shape
        top_k = expert_ids.shape[1]
        local_experts = w_gate.shape[0]
        capacity = tok_dev * top_k // num_devices
        rows = num_devices * capacity
        per_expert = rows // local_experts
        x_all = lax.all_gather(tokens, ep_axes, axis=0, tiled=True)
        all_experts = jnp.arange(num_devices * local_experts)
        gate_dense = jnp.sum(jnp.where(expert_ids[:, :, None] == all_experts[None, None, :], gate_weights[:, :, None], 0.0), axis=1)
        gate_send = gate_dense.reshape(tok_dev, num_devices, local_experts).transpose(1, 2, 0)
        gates = lax.all_to_all(gate_send, ep_axes, 0, 0, tiled=True)
        hit = jnp.any(gates > 0.0, axis=1)
        slot = jnp.where(hit, jnp.cumsum(hit.astype(jnp.int32), axis=1) - 1, -1)
        place = slot[:, None, :] == jnp.arange(capacity)[None, :, None]
        place_bf = place.astype(jnp.bfloat16)
        packed = jnp.einsum("sct,sth->sch", place_bf, x_all.reshape(num_devices, tok_dev, hidden), preferred_element_type=jnp.float32).astype(jnp.bfloat16)
        packed = packed.reshape(rows, hidden)
        gate_pack = jnp.sum(jnp.where(place[:, None], gates[:, :, None, :], 0.0), axis=3)
        gate_pack = gate_pack.transpose(1, 0, 2).reshape(local_experts, rows)
        chosen = gate_pack > 0.0
        rank = jnp.where(chosen, jnp.cumsum(chosen.astype(jnp.int32), axis=1) - 1, -1)
        pick = rank[:, None, :] == jnp.arange(per_expert)[None, :, None]
        pick_bf = pick.astype(jnp.bfloat16)
        pick_gates = jnp.sum(jnp.where(pick, gate_pack[:, None, :], 0.0), axis=2)
        x_exp = jnp.einsum("eir,rh->eih", pick_bf, packed, preferred_element_type=jnp.float32).astype(jnp.bfloat16)
        gate_act = jnp.einsum("lch,lhf->lcf", x_exp, w_gate, preferred_element_type=jnp.float32)
        up_act = jnp.einsum("lch,lhf->lcf", x_exp, w_up, preferred_element_type=jnp.float32)
        hidden_act = (jax.nn.silu(gate_act) * up_act).astype(jnp.bfloat16)
        out = jnp.einsum("lcf,lfh->lch", hidden_act, w_down, preferred_element_type=jnp.float32) * pick_gates[:, :, None]
        out_hi = lax.reduce_precision(out, 8, 7)
        out_lo = (out - out_hi).astype(jnp.bfloat16)
        out_hi = out_hi.astype(jnp.bfloat16)
        part = jnp.einsum("eir,eih->rh", pick_bf, out_hi, preferred_element_type=jnp.float32)
        part = part + jnp.einsum("eir,eih->rh", pick_bf, out_lo, preferred_element_type=jnp.float32)
        part = part.astype(jnp.bfloat16).reshape(num_devices, capacity, hidden)
        dense = jnp.einsum("sct,sch->sth", place_bf, part, preferred_element_type=jnp.float32).astype(jnp.bfloat16)
        moe_sum = lax.psum_scatter(dense.reshape(num_devices * tok_dev, hidden), ep_axes, scatter_dimension=0, tiled=True)
        return (tokens.astype(jnp.float32) + moe_sum.astype(jnp.float32)).astype(jnp.bfloat16)

    return jax.shard_map(local_layer, mesh=mesh, in_specs=(row_spec, row_spec, row_spec, w_spec, w_spec, w_spec), out_specs=row_spec, check_vma=False)
```

time: 342 us -> 416 us (1.22)
  waiting for transfers between devices: 41.1 us -> 239 us
  blocking collectives: 99.3 us -> 10.9 us
  local copies, waits for them, and re-layouts: 86.4 us -> 1.43 us
  matrix products: 56.1 us -> 140 us
  other arithmetic: 49.6 us -> 10.4 us
  between operations: 0.22 us -> 13.5 us
  starting transfers between devices: 9.16 us -> 0.04 us
    reduce_scatter x0 -> x1, waiting for transfers between devices: none -> 177 us  [local_layer(): lax.psum_scatter(dense.reshape(num_devices * tok_dev, hidden), ep_axes, s...]
    all_to_all x1, blocking collectives: 99.3 us -> 10.9 us  [local_layer(): gates = lax.all_to_all(gate_send, ep_axes, 0, 0, tiled=True)]
    dot_general x4 -> x7, matrix products: 56.1 us -> 140 us  [the longest x1 28 us: local_layer(): jnp.einsum('lcf,lfh->lch', hidden_act, w_down, preferred_element_type=jnp...]
    all_gather x0 -> x1, waiting for transfers between devices: none -> 61 us  [local_layer(): x_all = lax.all_gather(tokens, ep_axes, axis=0, tiled=True)]
    all_to_all x2 -> x0, waiting for transfers between devices: 41.1 us -> none  [the longest x1 41.1 us: local_layer(): recv_rows = lax.all_to_all(send_rows, ep_axes, 0, 0, tiled=True)]
    scatter-add x1 -> x0, other arithmetic: 34.1 us -> none  [local_layer(): jax.ops.segment_sum(weighted.reshape(-1, hidden), pick_rows.reshape(-1),...]
    unnamed x11 -> x7, local copies, waits for them, and re-layouts: 31.5 us -> 0.03 us
    another operation x3 -> x2, local copies, waits for them, and re-layouts: 30.8 us -> 0.22 us  [the longest x1 30.6 us: local_layer(): jax.ops.segment_sum(weighted.reshape(-1, hidden), pick_rows.reshape(-1),...]
  transfers between devices with their start and end apart: 2 -> 2, of which waited for: 1 -> 2; matrix products, arithmetic and copies ran while one was open for 21% -> 2% of each run, Pallas kernels for 0% -> 0%
where the time goes in v1:
time: 416 us; the launch traced here: 415 us
  waiting for transfers between devices  239 us (57%)
  matrix products  140 us (34%)
  between operations  13.5 us (3%)
  blocking collectives  10.9 us (3%)
  other arithmetic  10.4 us (2%)
    reduce_scatter x1, waiting for transfers between devices, local_layer(): lax.psum_scatter(dense.reshape(num_devices * tok_dev, hidden), ep_axes, s...  177 us
    all_gather x1, waiting for transfers between devices, local_layer(): x_all = lax.all_gather(tokens, ep_axes, axis=0, tiled=True)  61 us
    dot_general x1, matrix products, local_layer(): jnp.einsum('lcf,lfh->lch', hidden_act, w_down, preferred_element_type=jnp...  28 us
    dot_general x1, matrix products, local_layer(): jnp.einsum('eir,eih->rh', pick_bf, out_hi, preferred_element_type=jnp.flo...  27.6 us
    dot_general x1, matrix products, local_layer(): jnp.einsum('eir,eih->rh', pick_bf, out_lo, preferred_element_type=jnp.flo...  27.3 us
    dot_general x1, matrix products, local_layer(): jnp.einsum('eir,rh->eih', pick_bf, packed, preferred_element_type=jnp.flo...  21.4 us
    dot_general x1, matrix products, local_layer(): jnp.einsum('lch,lhf->lcf', x_exp, w_gate, preferred_element_type=jnp.floa...  17 us
    dot_general x1, matrix products, local_layer(): jnp.einsum('sct,sch->sth', place_bf, part, preferred_element_type=jnp.flo...  11.5 us
  transfers between devices with their start and end apart: 2, of which 2 were waited for; matrix products, arithmetic and copies ran while one was open for 2% of the time, Pallas kernels for 0%

profile of v1, /device:TPU:0, one launch (start us, length us, event | category | flops | bytes accessed | tf_op | source)
XLA Modules:
  0.0 415.5 jit_solution(15945308127021113659)
XLA Ops:
  6.5 0.7 all-gather.2.cloned.1.call-update
  7.3 0.8 select_reduce_fusion.2
  8.1 10.9 %all_to_all.5 = f32[16,4,256]{2,1,0:T(4,128)S(1)} all-to-all(f32[16,4,256]{2,1,0:T(4,128)S(1)} %bitcast.56), channel_id=1, replica_groups=mesh['ez'=2,'ey'=2,'ex'=4] {'ez','ey','ex'}, dimensions={0} | all-to-all | bytes 131072 | tf_op jit(solution)/shard_map/all_to_all | solution.py:25
  19.1 0.6 reduce-window.14
  19.7 0.2 slice_reduce_fusion.1
  19.9 0.1 bitcast_select_fusion.1
  20.0 0.7 iota_compare_fusion.8
  20.7 1.0 copy.28
  21.7 1.3 select_reduce_fusion.1
  23.0 1.2 reduce-window.16
  24.1 0.2 slice_reduce_fusion
  24.3 0.2 reduce-window.19
  24.6 0.1 add_bitcast_fusion
  24.7 2.8 select_reduce_fusion
  27.5 61.0 %all-gather.2.cloned.1.call-done = bf16[4096,2048]{1,0:T(8,128)(2,1)} async-done(((bf16[256,2048]{1,0:T(8,128)(2,1)}), bf16[4096,2048]{1,0:T(8,128)(2,1)}) %all-gather.2.cloned.1.call-update) | async-done | bytes 16777232 | tf_op jit(solution)/shard_map/all_gather | solution.py:21
  88.5 7.3 %convolution_convert_fusion.1 = bf16[16,128,2048]{2,1,0:T(8,128)(2,1)S(1)} fusion(bf16[16,256,2048]{2,1,0:T(8,128)(2,1)} %bitcast.51, s32[16,256]{1,0:T(8,128)S(1)} %bitcast_select_fusion.1), kind=kOutput, calls=%fused_computation.19 | convolution fusion | flops 2152202240 | bytes 25182208 | tf_op jit(solution)/shard_map/sct,sth->sch/dot_general | solution.py:30
  95.8 21.4 %fusion.11 = bf16[4,512,2048]{2,1,0:T(8,128)(2,1)} fusion(bf16[2048,2048,1]{1,0,2:T(8,128)(2,1)S(1)} %bitcast.53, s32[4,2048]{1,0:T(4,128)S(1)} %bitcast_select_fusion), kind=kOutput, calls=%fused_computation.18 | convolution fusion | flops 17188257792 | bytes 16809984 | tf_op jit(solution)/shard_map/eir,rh->eih/dot_general | solution.py:39
  117.2 17.0 %fusion.20 = f32[4,512,1024]{2,1,0:T(8,128)} fusion(bf16[4,512,2048]{2,1,0:T(8,128)(2,1)} %fusion.11, bf16[4,2048,1024]{2,1,0:T(8,128)(2,1)} %param.9), kind=kOutput, calls=%fused_computation.43 | convolution fusion | flops 8589934592 | bytes 33554432 | tf_op jit(solution)/shard_map/lch,lhf->lcf/dot_general | solution.py:40
  134.2 28.0 %fusion.12 = f32[4,512,2048]{2,1,0:T(8,128)} fusion(bf16[4,1024,2048]{2,1,0:T(8,128)(2,1)} %param.11, f32[4,512,1024]{2,1,0:T(8,128)} %fusion.20, bf16[4,512,2048]{2,1,0:T(8,128)(2,1)} %fusion.11, bf16[4,2048,1024]{2,1,0:T(8,128)(2,1)} %param.10), kind=kOutput, calls=%fused_computation.20 | convolution fusion | flops 17192452096 | bytes 67108864 | tf_op jit(solution)/shard_map/lcf,lfh->lch/dot_general | solution.py:43
  162.2 27.3 %fusion.2 = f32[2048,2048,1]{1,0,2:T(8,128)} fusion(f32[4,512,2048]{2,1,0:T(8,128)} %fusion.12, f32[4,512]{1,0:T(4,128)S(1)} %select_reduce_fusion, s32[4,2048]{1,0:T(4,128)S(1)} %bitcast_select_fusion), kind=kOutput, calls=%fused_computation.7 | convolution fusion | flops 17200840704 | bytes 33595392 | tf_op jit(solution)/shard_map/eir,eih->rh/dot_general | solution.py:48
  189.5 27.6 %fusion.1 = bf16[2048,2048]{1,0:T(8,128)(2,1)} fusion(f32[2048,2048,1]{1,0,2:T(8,128)} %fusion.2, f32[4,512,2048]{2,1,0:T(8,128)} %fusion.12, f32[4,512]{1,0:T(4,128)S(1)} %select_reduce_fusion, s32[4,2048]{1,0:T(4,128)S(1)} %bitcast_select_fusion), kind=kOutput, calls=%fused_computation.4 | convolution fusion | flops 17205035008 | bytes 41984000 | tf_op jit(solution)/shard_map/eir,eih->rh/dot_general | solution.py:47
  217.1 11.5 %convolution_convert_fusion = bf16[16,256,2048]{2,1,0:T(8,128)(2,1)} fusion(bf16[16,128,2048]{2,1,0:T(8,128)(2,1)} %bitcast.52, s32[16,256]{1,0:T(8,128)S(1)} %copy-done.2), kind=kOutput, calls=%fused_computation.10 | convolution fusion | flops 2156396544 | bytes 25182208 | tf_op jit(solution)/shard_map/sct,sch->sth/dot_general | solution.py:50
  228.6 177.4 %reduce-scatter.2.cloned.1.call-done = bf16[256,2048]{1,0:T(8,128)(2,1)} async-done(((bf16[4096,2048]{1,0:T(8,128)(2,1)}), bf16[256,2048]{1,0:T(8,128)(2,1)}) %reduce-scatter.2.cloned.1.call-update) | async-done | bytes 1048592 | tf_op jit(solution)/shard_map/reduce_scatter | solution.py:51
  406.0 2.6 add_convert_fusion
  (18 shorter events, 0.3 us)
Async XLA Ops:
  6.5 82.0 %all-gather.2.cloned.1.call-start = ((), (), s32[]{:S(2)}) async-start(), calls=%async_computation.2 | async-start | bytes 17825792 | tf_op jit(solution)/shard_map/all_gather | solution.py:21
  7.3 398.8 %reduce-scatter.2.cloned.1.call-start = ((), (), s32[]{:S(2)}) async-start(), calls=%async_computation.3 | async-start | bytes 17825792 | tf_op jit(solution)/shard_map/reduce_scatter | solution.py:51
  20.0 75.8 %copy-start.1 = (s32[16,256]{1,0:T(8,128)}, s32[16,256]{1,0:T(8,128)S(1)}, u32[]{:S(2)}) copy-start(s32[16,256]{1,0:T(8,128)S(1)} %bitcast_select_fusion.1) | copy-start | bytes 49156
  189.5 27.6 %copy-start.2 = (s32[16,256]{1,0:T(8,128)S(1)}, s32[16,256]{1,0:T(8,128)}, u32[]{:S(2)}) copy-start(s32[16,256]{1,0:T(8,128)} %copy-done.1) | copy-start | bytes 49156
  228.6 177.5 %copy-start = (bf16[256,2048]{1,0:T(8,128)(2,1)S(1)}, bf16[256,2048]{1,0:T(8,128)(2,1)}, u32[]{:S(2)}) copy-start(bf16[256,2048]{1,0:T(8,128)(2,1)} %param.6) | copy-start | bytes 3145732
Sparse Core Ops, SparseCore 0:
  9.6 78.8 all-gather.1
  228.7 177.2 reduce-scatter.1

commit v2 on v1

v2 whole, which is shorter than its diff:
```python
import math
import jax
import jax.numpy as jnp
from jax import lax
from jax.experimental import pallas as pl
from jax.experimental.pallas import tpu as pltpu
from jax.sharding import PartitionSpec as P

MESH = pl.DeviceIdType.MESH
CW = 256
ROW_PARTS = ((0, 96), (96, 80), (176, 80))
ALL = slice(None)
GATHER_STEPS = (
    (("x", (0, 0, 0), (0, 0, 1)), ("y", (0, 0, ALL), (0, 1, ALL)), ("z", (0, ALL, ALL), (1, ALL, ALL))),
    (("y", (0, 0, 0), (0, 1, 0)), ("z", (0, ALL, 0), (1, ALL, 0)), ("x", (ALL, ALL, 0), (ALL, ALL, 1))),
    (("z", (0, 0, 0), (1, 0, 0)), ("x", (ALL, 0, 0), (ALL, 0, 1)), ("y", (ALL, 0, ALL), (ALL, 1, ALL))),
)
SCATTER_STEPS = tuple(tuple((link, dst, src) for link, src, dst in steps[::-1]) for steps in GATHER_STEPS)
LANDING = ((1, 0, ALL, ALL), (1, 1, 0, ALL), (1, 1, 1, 0))


def moe_kernel(x_hbm, slot_row, slot_col, rank_row, rank_col, gate_row, w1_hbm, w3_hbm, w2_hbm, out_ref,
               g_buf, acc, sel, dense, hid, w13, w2, pair, x_exp, x_res, gate_col,
               step_send, step_recv, core_send, core_recv, x_sem, w13_sem, w2_sem, res_sem, ready):
    zb, yb, ex = lax.axis_index("ez"), lax.axis_index("ey"), lax.axis_index("ex")
    xb, cb = ex // 2, ex % 2
    peers = {
        "x": (zb, yb, (1 - xb) * 2 + cb),
        "y": (zb, 1 - yb, ex),
        "z": (1 - zb, yb, ex),
        "core": (zb, yb, xb * 2 + 1 - cb),
    }
    tok = x_hbm.shape[0]
    hidden = x_hbm.shape[1]
    chunks = hidden // CW
    experts, _, ff = w1_hbm.shape
    sources = slot_row.shape[0]
    rows = rank_col.shape[0]
    cap = rows // sources
    per_expert = rows // experts

    def xor(a, b):
        return a + b - 2 * a * b

    def source_of(rel):
        return (xor(zb, rel // 4 % 2) * 8 + xor(yb, rel // 2 % 2) * 4 + xor(xb, rel % 2) * 2 + xor(cb, rel // 8))

    def gather_copy(c, part, step):
        r0, n = ROW_PARTS[part]
        link, src, dst = GATHER_STEPS[part][step]
        return pltpu.make_async_remote_copy(
            g_buf.at[(c, 0) + src + (pl.ds(r0, n),)], g_buf.at[(c, 0) + dst + (pl.ds(r0, n),)],
            step_send.at[c, part, step], step_recv.at[c, part, step], device_id=peers[link], device_id_type=MESH)

    def gather_core(c):
        return pltpu.make_async_remote_copy(g_buf.at[c, 0], g_buf.at[c, 1], core_send.at[c], core_recv.at[c],
                                            device_id=peers["core"], device_id_type=MESH)

    def scatter_core(k):
        return pltpu.make_async_remote_copy(dense.at[k % 2, 1], g_buf.at[k, 0], core_send.at[k], core_recv.at[k],
                                            device_id=peers["core"], device_id_type=MESH)

    def scatter_copy(k, part, step):
        r0, n = ROW_PARTS[part]
        link, src, _ = SCATTER_STEPS[part][step]
        return pltpu.make_async_remote_copy(
            g_buf.at[(k, 0) + src + (pl.ds(r0, n),)], g_buf.at[(k,) + LANDING[step] + (pl.ds(r0, n),)],
            step_send.at[k, part, step], step_recv.at[k, part, step], device_id=peers[link], device_id_type=MESH)

    def x_copy(c):
        cols = pl.ds(pl.multiple_of(c * CW, CW), CW)
        return pltpu.make_async_copy(x_hbm.at[:, cols], g_buf.at[c, 0, 0, 0, 0], x_sem.at[c])

    def w13_copies(i):
        c, e, b = i // experts, i % experts, i % 2
        k_rows = pl.ds(pl.multiple_of(c * CW, CW), CW)
        return (pltpu.make_async_copy(w1_hbm.at[e, k_rows], w13.at[b, 0], w13_sem.at[b, 0]),
                pltpu.make_async_copy(w3_hbm.at[e, k_rows], w13.at[b, 1], w13_sem.at[b, 1]))

    def w2_copy(i):
        k, e, b = i // experts, i % experts, i % 2
        cols = pl.ds(pl.multiple_of(k * CW, CW), CW)
        return pltpu.make_async_copy(w2_hbm.at[e, :, cols], w2.at[b], w2_sem.at[b])

    def each(parts, fn):
        for part in parts:
            fn(part)

    PARTS = range(len(ROW_PARTS))

    for c in range(chunks):
        x_copy(c).start()
    res_copy = pltpu.make_async_copy(x_hbm, x_res, res_sem)
    res_copy.start()
    for i in range(2):
        for copy in w13_copies(i):
            copy.start()
        w2_copy(i).start()
    barrier = pltpu.get_barrier_semaphore()
    for peer in peers.values():
        pl.semaphore_signal(barrier, inc=1, device_id=peer, device_id_type=MESH)
    pl.semaphore_wait(barrier, len(peers))

    def start_first(c):
        x_copy(c).wait()
        each(PARTS, lambda p: gather_copy(c, p, 0).start())

    def advance(c, step):
        def one(p):
            gather_copy(c, p, step - 1).wait_recv()
            gather_copy(c, p, step).start()
        each(PARTS, one)

    def to_core(c):
        each(PARTS, lambda p: gather_copy(c, p, 2).wait_recv())
        gather_core(c).start()

    def pack(c):
        @pl.loop(0, sources)
        def _(rel):
            s = source_of(rel)
            iota = lax.broadcasted_iota(jnp.int32, (cap, tok), 0)
            one_hot = jnp.where(slot_row[pl.ds(s, 1), :] == iota, 1.0, 0.0).astype(jnp.bfloat16)
            block = g_buf[c, rel // 8, rel // 4 % 2, rel // 2 % 2, rel % 2]
            packed = jnp.dot(one_hot, block, preferred_element_type=jnp.float32)
            pair[0, pl.ds(pl.multiple_of(s * cap, cap), cap), :] = packed.astype(jnp.bfloat16)

    def up_project(c, e0, e1):
        @pl.loop(e0, e1)
        def _(e):
            i = c * experts + e
            for copy in w13_copies(i):
                copy.wait()
            erows = pl.ds(pl.multiple_of(e * per_expert, per_expert), per_expert)
            x_exp[...] = jnp.dot(sel[erows, :], pair[0], preferred_element_type=jnp.float32).astype(jnp.bfloat16)
            for j in range(2):
                prod = jnp.dot(x_exp[...], w13[i % 2, j], preferred_element_type=jnp.float32)

                @pl.when(c == 0)
                def _():
                    acc[j, erows, :] = prod

                @pl.when(c > 0)
                def _():
                    acc[j, erows, :] += prod

            @pl.when(i + 2 < chunks * experts)
            def _():
                for copy in w13_copies(i + 2):
                    copy.start()

    def build_pick():
        tile = 128

        @pl.loop(0, rows // tile)
        def _(t):
            e = t * tile // per_expert
            iota = lax.broadcasted_iota(jnp.int32, (tile, rows), 0) + t * tile % per_expert
            mask = rank_row[pl.ds(e, 1), :] == iota
            trows = pl.ds(pl.multiple_of(t * tile, tile), tile)
            sel[trows, :] = jnp.where(mask, 1.0, 0.0).astype(jnp.bfloat16)
            gate_col[trows, :] = jnp.sum(jnp.where(mask, gate_row[pl.ds(e, 1), :], 0.0), axis=1, keepdims=True)

    start_first(0)
    start_first(1)
    advance(0, 1)
    start_first(2)
    advance(1, 1)
    advance(0, 2)
    build_pick()
    start_first(3)
    advance(2, 1)
    advance(1, 2)
    to_core(0)

    @pl.loop(1, chunks + 1)
    def _(k):
        @pl.when(k + 3 < chunks)
        def _():
            start_first(k + 3)

        @pl.when(k + 2 < chunks)
        def _():
            advance(k + 2, 1)

        @pl.when(k + 1 < chunks)
        def _():
            advance(k + 1, 2)

        gather_core(k - 1).wait_recv()
        pack(k - 1)
        up_project(k - 1, 0, experts // 2)

        @pl.when(k < chunks)
        def _():
            to_core(k)

        up_project(k - 1, experts // 2, experts)

    @pl.loop(0, chunks)
    def _(c):
        for p in PARTS:
            for step in range(3):
                gather_copy(c, p, step).wait_send()
        gather_core(c).wait_send()

    for peer in peers.values():
        pl.semaphore_signal(ready, inc=1, device_id=peer, device_id_type=MESH)

    @pl.loop(0, rows // 128)
    def _(t):
        trows = pl.ds(pl.multiple_of(t * 128, 128), 128)
        hid[trows, :] = (jax.nn.silu(acc[0, trows, :]) * acc[1, trows, :]).astype(jnp.bfloat16)
        iota = lax.broadcasted_iota(jnp.int32, (128, per_expert), 1)
        for e in range(experts):
            mask = rank_col[trows, e:e + 1] == iota
            sel[trows, e * per_expert:(e + 1) * per_expert] = jnp.where(mask, 1.0, 0.0).astype(jnp.bfloat16)

    res_copy.wait()
    pl.semaphore_wait(ready, len(peers))

    def add_into(dst, others):
        total = dst[...].astype(jnp.float32)
        for other in others:
            total = total + other[...].astype(jnp.float32)
        dst[...] = total.astype(jnp.bfloat16)

    def sum_core(k):
        scatter_core(k).wait_recv()

        @pl.loop(0, 8)
        def _(j):
            idx = (j // 4, j // 2 % 2, j % 2)
            add_into(g_buf.at[(k, 0) + idx], [dense.at[(k % 2, 0) + idx]])

    def sum_first(k):
        for p in PARTS:
            scatter_copy(k, p, 0).wait_recv()
            r0, n = ROW_PARTS[p]
            add_into(g_buf.at[(k, 0) + SCATTER_STEPS[p][0][2] + (pl.ds(r0, n),)], [g_buf.at[(k,) + LANDING[0] + (pl.ds(r0, n),)]])

    def sum_second(k):
        for p in PARTS:
            scatter_copy(k, p, 1).wait_recv()
            r0, n = ROW_PARTS[p]
            add_into(g_buf.at[(k, 0) + SCATTER_STEPS[p][2][1] + (pl.ds(r0, n),)], [g_buf.at[k, 1, 1, 0, 1, pl.ds(r0, n)]])

    def finish(k):
        for p in PARTS:
            scatter_copy(k, p, 2).wait_recv()
        cols = pl.ds(pl.multiple_of(k * CW, CW), CW)
        moe = g_buf[k, 0, 0, 0, 0].astype(jnp.float32) + g_buf[k, 1, 1, 0, 0].astype(jnp.float32) + g_buf[k, 1, 1, 1, 0].astype(jnp.float32)
        out_ref[:, cols] = (x_res[:, cols].astype(jnp.float32) + moe).astype(jnp.bfloat16)

    def down_project(k):
        @pl.loop(0, experts)
        def _(e):
            i = k * experts + e
            w2_copy(i).wait()
            erows = pl.ds(pl.multiple_of(e * per_expert, per_expert), per_expert)
            o = jnp.dot(hid[erows, :], w2[i % 2], preferred_element_type=jnp.float32) * gate_col[erows, :]
            hi = o.astype(jnp.bfloat16)
            pair[0, erows, :] = hi
            pair[1, erows, :] = (o - hi.astype(jnp.float32)).astype(jnp.bfloat16)

            @pl.when(i + 2 < chunks * experts)
            def _():
                w2_copy(i + 2).start()

    def combine(k):
        @pl.loop(0, sources // 2)
        def _(m):
            mrows = pl.ds(pl.multiple_of(m * 2 * cap, 2 * cap), 2 * cap)
            pick = sel[mrows, :]
            part = jnp.dot(pick, pair[0], preferred_element_type=jnp.float32)
            part = part + jnp.dot(pick, pair[1], preferred_element_type=jnp.float32)
            part = part.astype(jnp.bfloat16)
            rz, ry, rx = xor(m // 4, zb), xor(m // 2 % 2, yb), xor(m % 2, xb)
            for core in range(2):
                s = m * 2 + core
                slots = slot_col[pl.ds(pl.multiple_of(s * tok, tok), tok), :]
                place = jnp.where(slots == lax.broadcasted_iota(jnp.int32, (tok, cap), 1), 1.0, 0.0).astype(jnp.bfloat16)
                spread = jnp.dot(place, part[core * cap:(core + 1) * cap, :], preferred_element_type=jnp.float32)
                dense[k % 2, xor(core, cb), rz, ry, rx] = spread.astype(jnp.bfloat16)

    @pl.loop(0, chunks + 4)
    def _(k):
        @pl.when((k >= 1) & (k <= chunks))
        def _():
            sum_core(k - 1)

        @pl.when((k >= 2) & (k <= chunks + 1))
        def _():
            sum_first(k - 2)

        @pl.when((k >= 3) & (k <= chunks + 2))
        def _():
            sum_second(k - 3)

        @pl.when((k >= 1) & (k <= chunks))
        def _():
            each(PARTS, lambda p: scatter_copy(k - 1, p, 0).start())

        @pl.when((k >= 2) & (k <= chunks + 1))
        def _():
            each(PARTS, lambda p: scatter_copy(k - 2, p, 1).start())

        @pl.when((k >= 3) & (k <= chunks + 2))
        def _():
            each(PARTS, lambda p: scatter_copy(k - 3, p, 2).start())

        @pl.when(k >= 4)
        def _():
            finish(k - 4)

        @pl.when(k < chunks)
        def _():
            down_project(k)

            @pl.when(k >= 2)
            def _():
                scatter_core(k - 2).wait_send()

            combine(k)
            scatter_core(k).start()

    for k in (chunks - 2, chunks - 1):
        scatter_core(k).wait_send()

    @pl.loop(0, chunks)
    def _(k):
        for p in PARTS:
            for step in range(3):
                scatter_copy(k, p, step).wait_send()


def moe_call(tokens, slot_row, slot_col, rank_row, rank_col, gate_row, w_gate, w_up, w_down):
    tok, hidden = tokens.shape
    experts, _, ff = w_gate.shape
    rows = rank_col.shape[0]
    chunks = hidden // CW
    bf16, f32 = jnp.bfloat16, jnp.float32
    vmem = pl.BlockSpec(memory_space=pltpu.VMEM)
    hbm = pl.BlockSpec(memory_space=pl.ANY)
    dma = pltpu.SemaphoreType.DMA
    return pl.pallas_call(
        moe_kernel,
        out_shape=jax.ShapeDtypeStruct((tok, hidden), bf16),
        in_specs=[hbm, vmem, vmem, vmem, vmem, vmem, hbm, hbm, hbm],
        out_specs=vmem,
        scratch_shapes=[
            pltpu.VMEM((chunks, 2, 2, 2, 2, tok, CW), bf16),
            pltpu.VMEM((2, rows, ff), f32),
            pltpu.VMEM((rows, rows), bf16),
            pltpu.VMEM((2, 2, 2, 2, 2, tok, CW), bf16),
            pltpu.VMEM((rows, ff), bf16),
            pltpu.VMEM((2, 2, CW, ff), bf16),
            pltpu.VMEM((2, ff, CW), bf16),
            pltpu.VMEM((2, rows, CW), bf16),
            pltpu.VMEM((rows // experts, CW), bf16),
            pltpu.VMEM((tok, hidden), bf16),
            pltpu.VMEM((rows, 1), f32),
            dma((chunks, 3, 3)), dma((chunks, 3, 3)), dma((chunks,)), dma((chunks,)), dma((chunks,)),
            dma((2, 2)), dma((2,)), dma, pltpu.SemaphoreType.REGULAR,
        ],
        compiler_params=pltpu.CompilerParams(collective_id=0, has_side_effects=True, vmem_limit_bytes=67043328),
    )(tokens, slot_row, slot_col, rank_row, rank_col, gate_row, w_gate, w_up, w_down)


def solution(mesh):
    ep_axes = tuple(mesh.axis_names)
    num_devices = math.prod(mesh.shape[axis_name] for axis_name in ep_axes)
    row_spec = P(ep_axes, None)
    w_spec = P(ep_axes, None, None)

    def local_layer(tokens, expert_ids, gate_weights, w_gate, w_up, w_down):
        tok_dev, hidden = tokens.shape
        top_k = expert_ids.shape[1]
        local_experts = w_gate.shape[0]
        capacity = tok_dev * top_k // num_devices
        rows = num_devices * capacity
        all_experts = jnp.arange(num_devices * local_experts)
        gate_dense = jnp.sum(jnp.where(expert_ids[:, :, None] == all_experts[None, None, :], gate_weights[:, :, None], 0.0), axis=1)
        gate_send = gate_dense.reshape(tok_dev, num_devices, local_experts).transpose(1, 2, 0)
        gates = lax.all_to_all(gate_send, ep_axes, 0, 0, tiled=True)
        hit = jnp.any(gates > 0.0, axis=1)
        slot = jnp.where(hit, jnp.cumsum(hit.astype(jnp.int32), axis=1) - 1, -1)
        place = slot[:, None, :] == jnp.arange(capacity)[None, :, None]
        gate_pack = jnp.sum(jnp.where(place[:, None], gates[:, :, None, :], 0.0), axis=3)
        gate_pack = gate_pack.transpose(1, 0, 2).reshape(local_experts, rows)
        chosen = gate_pack > 0.0
        rank = jnp.where(chosen, jnp.cumsum(chosen.astype(jnp.int32), axis=1) - 1, -1)
        return moe_call(tokens, slot, slot.reshape(-1, 1), rank, rank.T, gate_pack, w_gate, w_up, w_down)

    return jax.shard_map(local_layer, mesh=mesh, in_specs=(row_spec, row_spec, row_spec, w_spec, w_spec, w_spec), out_specs=row_spec, check_vma=False)
```

time: 416 us -> 287 us (0.69)
  Pallas kernels: 0 us -> 262 us
  waiting for transfers between devices: 239 us -> 0 us
  matrix products: 140 us -> 0 us
  between operations: 13.5 us -> 0.08 us
  local copies, waits for them, and re-layouts: 1.43 us -> 6.76 us
  other arithmetic: 10.4 us -> 6.2 us
    pallas_call x0 -> x1, Pallas kernels: none -> 262 us  [moe_call(): pl.pallas_call(moe_kernel, out_shape=jax.ShapeDtypeStruct((tok, hidden),...]
    reduce_scatter x1 -> x0, waiting for transfers between devices: 177 us -> none  [local_layer(): lax.psum_scatter(dense.reshape(num_devices * tok_dev, hidden), ep_axes, s...]
    dot_general x7 -> x0, matrix products: 140 us -> none  [the longest x1 28 us: local_layer(): jnp.einsum('lcf,lfh->lch', hidden_act, w_down, preferred_element_type=jnp...]
    all_gather x1 -> x0, waiting for transfers between devices: 61 us -> none  [local_layer(): x_all = lax.all_gather(tokens, ep_axes, axis=0, tiled=True)]
    unnamed x7 -> x8, local copies, waits for them, and re-layouts: 0.03 us -> 4.34 us
  transfers between devices with their start and end apart: 2 -> 0, of which waited for: 2 -> 0; matrix products, arithmetic and copies ran while one was open for 2% -> 0% of each run, Pallas kernels for 0% -> 0%
where the time goes in v2:
time: 287 us; the launch traced here: 286 us
  Pallas kernels  262 us (91%)
  blocking collectives  10.9 us (4%)
  local copies, waits for them, and re-layouts  6.76 us (2%)
  other arithmetic  6.2 us (2%)
    pallas_call x1, Pallas kernels, moe_call(): pl.pallas_call(moe_kernel, out_shape=jax.ShapeDtypeStruct((tok, hidden),...  262 us
    all_to_all x1, blocking collectives, local_layer(): gates = lax.all_to_all(gate_send, ep_axes, 0, 0, tiled=True)  10.9 us

profile of v2, /device:TPU:0, one launch (start us, length us, event | category | flops | bytes accessed | tf_op | source)
XLA Modules:
  0.0 286.4 jit_solution(4175012231369825332)
XLA Ops:
  0.0 0.8 select_reduce_fusion.1
  0.8 10.9 %all_to_all.5 = f32[16,4,256]{2,1,0:T(4,128)S(1)} all-to-all(f32[16,4,256]{2,1,0:T(4,128)S(1)} %bitcast.40), channel_id=1, replica_groups=mesh['ez'=2,'ey'=2,'ex'=4] {'ez','ey','ex'}, dimensions={0} | all-to-all | bytes 131072 | tf_op jit(solution)/shard_map/all_to_all | solution.py:385
  11.7 0.1 compare_reduce_fusion
  11.8 0.6 reduce-window.14
  12.4 0.2 slice_reduce_fusion.1
  12.6 0.1 bitcast_select_fusion.2.slot_row
  12.7 0.0 copy-start.1
  12.7 0.1 add_add_fusion
  12.8 0.5 copy-done.1
  13.3 0.3 iota_compare_fusion
  13.6 1.3 select_reduce_fusion
  14.9 0.8 copy.39
  15.8 1.2 reduce-window.16
  16.9 0.2 slice_reduce_fusion
  17.2 0.2 reduce-window.19
  17.4 0.1 add_bitcast_fusion
  17.4 0.6 copy.50
  18.1 0.0 copy-start
  18.1 1.3 copy.35.rank_col
  19.4 0.0 copy-done
  19.5 0.6 copy.33
  20.1 1.6 bitcast_select_fusion.slot_col
  21.7 262.4 %shard_map.64 = bf16[256,2048]{1,0:T(8,128)(2,1)} custom-call(bf16[256,2048]{1,0:T(8,128)(2,1)} %x_hbm.1, s32[16,256]{1,0:T(8,128)} %copy-done.1, s32[4096,1]{1,0:T(8,128)} %bitcast_select_fusion.slot_col, s32[4,2048]{1,0:T(4,128)} %copy-done, s32[2048,4]{1,0:T(8,128)} %copy.35.rank_col, f32[4,2048]{1,0:T(4,128)} %bitcast.41, bf16[4,2048,1024]{2,1,0:T(8,128)(2,1)} %w1_hbm.1, ...), custom_call_target="tpu_custom_call" | custom-call | tf_op jit(solution)/shard_map/pallas_call | solution.py:346
  284.1 2.3 copy.53
  (9 shorter events, 0.1 us)
Async XLA Ops:
  12.7 0.6 copy-start.1
  18.1 1.4 copy-start

commit v3 on v2

--- a/solution.py
+++ b/solution.py
@@ -101,20 +101,24 @@
         pl.semaphore_signal(barrier, inc=1, device_id=peer, device_id_type=MESH)
     pl.semaphore_wait(barrier, len(peers))
 
+    @jax.named_scope("start_first")
     def start_first(c):
         x_copy(c).wait()
         each(PARTS, lambda p: gather_copy(c, p, 0).start())
 
+    @jax.named_scope("advance")
     def advance(c, step):
         def one(p):
             gather_copy(c, p, step - 1).wait_recv()
             gather_copy(c, p, step).start()
         each(PARTS, one)
 
+    @jax.named_scope("to_core")
     def to_core(c):
         each(PARTS, lambda p: gather_copy(c, p, 2).wait_recv())
         gather_core(c).start()
 
+    @jax.named_scope("pack")
     def pack(c):
         @pl.loop(0, sources)
         def _(rel):
@@ -125,6 +129,7 @@
             packed = jnp.dot(one_hot, block, preferred_element_type=jnp.float32)
             pair[0, pl.ds(pl.multiple_of(s * cap, cap), cap), :] = packed.astype(jnp.bfloat16)
 
+    @jax.named_scope("up_project")
     def up_project(c, e0, e1):
         @pl.loop(e0, e1)
         def _(e):
@@ -134,21 +139,15 @@
             erows = pl.ds(pl.multiple_of(e * per_expert, per_expert), per_expert)
             x_exp[...] = jnp.dot(sel[erows, :], pair[0], preferred_element_type=jnp.float32).astype(jnp.bfloat16)
             for j in range(2):
-                prod = jnp.dot(x_exp[...], w13[i % 2, j], preferred_element_type=jnp.float32)
-
-                @pl.when(c == 0)
-                def _():
-                    acc[j, erows, :] = prod
-
-                @pl.when(c > 0)
-                def _():
-                    acc[j, erows, :] += prod
+                for n in range(0, ff, CW):
+                    acc[j, erows, n:n + CW] += jnp.dot(x_exp[...], w13[i % 2, j, :, n:n + CW], preferred_element_type=jnp.float32)
 
             @pl.when(i + 2 < chunks * experts)
             def _():
                 for copy in w13_copies(i + 2):
                     copy.start()
 
+    @jax.named_scope("build_pick")
     def build_pick():
         tile = 128
 
@@ -161,13 +160,22 @@
             sel[trows, :] = jnp.where(mask, 1.0, 0.0).astype(jnp.bfloat16)
             gate_col[trows, :] = jnp.sum(jnp.where(mask, gate_row[pl.ds(e, 1), :], 0.0), axis=1, keepdims=True)
 
+    @jax.named_scope("clear_sums")
+    def clear_sums():
+        @pl.loop(0, rows // 64)
+        def _(t):
+            trows = pl.ds(pl.multiple_of(t * 64, 64), 64)
+            for j in range(2):
+                acc[j, trows, :] = jnp.zeros((64, ff), jnp.float32)
+
     start_first(0)
     start_first(1)
+    clear_sums()
     advance(0, 1)
     start_first(2)
+    build_pick()
     advance(1, 1)
     advance(0, 2)
-    build_pick()
     start_first(3)
     advance(2, 1)
     advance(1, 2)
@@ -225,6 +233,7 @@
             total = total + other[...].astype(jnp.float32)
         dst[...] = total.astype(jnp.bfloat16)
 
+    @jax.named_scope("sum_core")
     def sum_core(k):
         scatter_core(k).wait_recv()
 
@@ -233,18 +242,21 @@
             idx = (j // 4, j // 2 % 2, j % 2)
             add_into(g_buf.at[(k, 0) + idx], [dense.at[(k % 2, 0) + idx]])
 
+    @jax.named_scope("sum_first")
     def sum_first(k):
         for p in PARTS:
             scatter_copy(k, p, 0).wait_recv()
             r0, n = ROW_PARTS[p]
             add_into(g_buf.at[(k, 0) + SCATTER_STEPS[p][0][2] + (pl.ds(r0, n),)], [g_buf.at[(k,) + LANDING[0] + (pl.ds(r0, n),)]])
 
+    @jax.named_scope("sum_second")
     def sum_second(k):
         for p in PARTS:
             scatter_copy(k, p, 1).wait_recv()
             r0, n = ROW_PARTS[p]
             add_into(g_buf.at[(k, 0) + SCATTER_STEPS[p][2][1] + (pl.ds(r0, n),)], [g_buf.at[k, 1, 1, 0, 1, pl.ds(r0, n)]])
 
+    @jax.named_scope("finish")
     def finish(k):
         for p in PARTS:
             scatter_copy(k, p, 2).wait_recv()
@@ -252,6 +264,10 @@
         moe = g_buf[k, 0, 0, 0, 0].astype(jnp.float32) + g_buf[k, 1, 1, 0, 0].astype(jnp.float32) + g_buf[k, 1, 1, 1, 0].astype(jnp.float32)
         out_ref[:, cols] = (x_res[:, cols].astype(jnp.float32) + moe).astype(jnp.bfloat16)
 
+    def start_scatter(k):
+        each(PARTS, lambda p: scatter_copy(k, p, 0).start())
+
+    @jax.named_scope("down_project")
     def down_project(k):
         @pl.loop(0, experts)
         def _(e):
@@ -267,9 +283,14 @@
             def _():
                 w2_copy(i + 2).start()
 
+    @jax.named_scope("combine")
     def combine(k):
         @pl.loop(0, sources // 2)
         def _(m):
+            @pl.when((m == 1) & (k >= 1))
+            def _():
+                start_scatter(k - 1)
+
             mrows = pl.ds(pl.multiple_of(m * 2 * cap, 2 * cap), 2 * cap)
             pick = sel[mrows, :]
             part = jnp.dot(pick, pair[0], preferred_element_type=jnp.float32)
@@ -285,44 +306,46 @@
 
     @pl.loop(0, chunks + 4)
     def _(k):
+        @pl.when((k >= 2) & (k <= chunks + 1))
+        def _():
+            sum_first(k - 2)
+
+        @pl.when((k >= 3) & (k <= chunks + 2))
+        def _():
+            sum_second(k - 3)
+
+        @pl.when((k >= 2) & (k <= chunks + 1))
+        def _():
+            each(PARTS, lambda p: scatter_copy(k - 2, p, 1).start())
+
+        @pl.when((k >= 3) & (k <= chunks + 2))
+        def _():
+            each(PARTS, lambda p: scatter_copy(k - 3, p, 2).start())
+
+        @pl.when(k < chunks)
+        def _():
+            down_project(k)
+
         @pl.when((k >= 1) & (k <= chunks))
         def _():
             sum_core(k - 1)
 
-        @pl.when((k >= 2) & (k <= chunks + 1))
-        def _():
-            sum_first(k - 2)
-
-        @pl.when((k >= 3) & (k <= chunks + 2))
-        def _():
-            sum_second(k - 3)
-
-        @pl.when((k >= 1) & (k <= chunks))
-        def _():
-            each(PARTS, lambda p: scatter_copy(k - 1, p, 0).start())
-
-        @pl.when((k >= 2) & (k <= chunks + 1))
-        def _():
-            each(PARTS, lambda p: scatter_copy(k - 2, p, 1).start())
-
-        @pl.when((k >= 3) & (k <= chunks + 2))
-        def _():
-            each(PARTS, lambda p: scatter_copy(k - 3, p, 2).start())
-
-        @pl.when(k >= 4)
-        def _():
-            finish(k - 4)
+        @pl.when(k == chunks)
+        def _():
+            start_scatter(k - 1)
 
         @pl.when(k < chunks)
         def _():
-            down_project(k)
-
             @pl.when(k >= 2)
             def _():
                 scatter_core(k - 2).wait_send()
 
             combine(k)
             scatter_core(k).start()
+
+        @pl.when(k >= 4)
+        def _():
+            finish(k - 4)
 
     for k in (chunks - 2, chunks - 1):
         scatter_core(k).wait_send()

time: 287 us -> 253 us (0.88)
  Pallas kernels: 262 us -> 228 us
    pallas_call x1, Pallas kernels: 262 us -> 228 us  [moe_call(): pl.pallas_call(moe_kernel, out_shape=jax.ShapeDtypeStruct((tok, hidden),...]
where the time goes in v3:
time: 253 us; the launch traced here: 252 us
  Pallas kernels  228 us (90%)
  blocking collectives  10.9 us (4%)
  local copies, waits for them, and re-layouts  6.76 us (3%)
  other arithmetic  6.2 us (2%)
    pallas_call x1, Pallas kernels, moe_call(): pl.pallas_call(moe_kernel, out_shape=jax.ShapeDtypeStruct((tok, hidden),...  228 us
    all_to_all x1, blocking collectives, local_layer(): gates = lax.all_to_all(gate_send, ep_axes, 0, 0, tiled=True)  10.9 us

profile of v3, /device:TPU:0, one launch (start us, length us, event | category | flops | bytes accessed | tf_op | source)
XLA Modules:
  0.0 252.3 jit_solution(13120551363652288083)
XLA Ops:
  0.0 0.8 select_reduce_fusion.1
  0.8 10.9 %all_to_all.5 = f32[16,4,256]{2,1,0:T(4,128)S(1)} all-to-all(f32[16,4,256]{2,1,0:T(4,128)S(1)} %bitcast.40), channel_id=1, replica_groups=mesh['ez'=2,'ey'=2,'ex'=4] {'ez','ey','ex'}, dimensions={0} | all-to-all | bytes 131072 | tf_op jit(solution)/shard_map/all_to_all | solution.py:408
  11.7 0.1 compare_reduce_fusion
  11.8 0.6 reduce-window.14
  12.4 0.2 slice_reduce_fusion.1
  12.6 0.1 bitcast_select_fusion.2.slot_row
  12.7 0.0 copy-start.1
  12.7 0.1 add_add_fusion
  12.8 0.5 copy-done.1
  13.3 0.3 iota_compare_fusion
  13.6 1.3 select_reduce_fusion
  14.9 0.8 copy.39
  15.8 1.2 reduce-window.16
  16.9 0.2 slice_reduce_fusion
  17.2 0.2 reduce-window.19
  17.4 0.1 add_bitcast_fusion
  17.4 0.6 copy.50
  18.1 0.0 copy-start
  18.1 1.3 copy.35.rank_col
  19.4 0.0 copy-done
  19.5 0.6 copy.33
  20.1 1.6 bitcast_select_fusion.slot_col
  21.7 228.3 %shard_map.64 = bf16[256,2048]{1,0:T(8,128)(2,1)} custom-call(bf16[256,2048]{1,0:T(8,128)(2,1)} %x_hbm.1, s32[16,256]{1,0:T(8,128)} %copy-done.1, s32[4096,1]{1,0:T(8,128)} %bitcast_select_fusion.slot_col, s32[4,2048]{1,0:T(4,128)} %copy-done, s32[2048,4]{1,0:T(8,128)} %copy.35.rank_col, f32[4,2048]{1,0:T(4,128)} %bitcast.41, bf16[4,2048,1024]{2,1,0:T(8,128)(2,1)} %w1_hbm.1, ...), custom_call_target="tpu_custom_call" | custom-call | tf_op jit(solution)/shard_map/pallas_call | solution.py:369
  250.0 2.3 copy.53
  (9 shorter events, 0.1 us)
Async XLA Ops:
  12.7 0.6 copy-start.1
  18.1 1.4 copy-start

commit v4 on v3

--- a/solution.py
+++ b/solution.py
@@ -20,7 +20,7 @@
 
 
 def moe_kernel(x_hbm, slot_row, slot_col, rank_row, rank_col, gate_row, w1_hbm, w3_hbm, w2_hbm, out_ref,
-               g_buf, acc, sel, dense, hid, w13, w2, pair, x_exp, x_res, gate_col,
+               g_buf, acc, sel, dense, hid, w13, w2, pair, x_exp, part, x_res, gate_col,
                step_send, step_recv, core_send, core_recv, x_sem, w13_sem, w2_sem, res_sem, ready):
     zb, yb, ex = lax.axis_index("ez"), lax.axis_index("ey"), lax.axis_index("ex")
     xb, cb = ex // 2, ex % 2
@@ -71,16 +71,15 @@
         cols = pl.ds(pl.multiple_of(c * CW, CW), CW)
         return pltpu.make_async_copy(x_hbm.at[:, cols], g_buf.at[c, 0, 0, 0, 0], x_sem.at[c])
 
-    def w13_copies(i):
-        c, e, b = i // experts, i % experts, i % 2
+    def w13_copies(c, e):
+        b = e % 2
         k_rows = pl.ds(pl.multiple_of(c * CW, CW), CW)
         return (pltpu.make_async_copy(w1_hbm.at[e, k_rows], w13.at[b, 0], w13_sem.at[b, 0]),
                 pltpu.make_async_copy(w3_hbm.at[e, k_rows], w13.at[b, 1], w13_sem.at[b, 1]))
 
-    def w2_copy(i):
-        k, e, b = i // experts, i % experts, i % 2
+    def w2_copy(k, e):
         cols = pl.ds(pl.multiple_of(k * CW, CW), CW)
-        return pltpu.make_async_copy(w2_hbm.at[e, :, cols], w2.at[b], w2_sem.at[b])
+        return pltpu.make_async_copy(w2_hbm.at[e, :, cols], w2.at[e % 2], w2_sem.at[e % 2])
 
     def each(parts, fn):
         for part in parts:
@@ -92,10 +91,10 @@
         x_copy(c).start()
     res_copy = pltpu.make_async_copy(x_hbm, x_res, res_sem)
     res_copy.start()
-    for i in range(2):
-        for copy in w13_copies(i):
+    for e in range(2):
+        for copy in w13_copies(0, e):
             copy.start()
-        w2_copy(i).start()
+        w2_copy(0, e).start()
     barrier = pltpu.get_barrier_semaphore()
     for peer in peers.values():
         pl.semaphore_signal(barrier, inc=1, device_id=peer, device_id_type=MESH)
@@ -120,32 +119,37 @@
 
     @jax.named_scope("pack")
     def pack(c):
-        @pl.loop(0, sources)
-        def _(rel):
-            s = source_of(rel)
-            iota = lax.broadcasted_iota(jnp.int32, (cap, tok), 0)
-            one_hot = jnp.where(slot_row[pl.ds(s, 1), :] == iota, 1.0, 0.0).astype(jnp.bfloat16)
-            block = g_buf[c, rel // 8, rel // 4 % 2, rel // 2 % 2, rel % 2]
-            packed = jnp.dot(one_hot, block, preferred_element_type=jnp.float32)
-            pair[0, pl.ds(pl.multiple_of(s * cap, cap), cap), :] = packed.astype(jnp.bfloat16)
+        @pl.loop(0, sources // 4)
+        def _(q):
+            for u in range(4):
+                rel = q * 4 + u
+                s = source_of(rel)
+                iota = lax.broadcasted_iota(jnp.int32, (cap, tok), 0)
+                one_hot = jnp.where(slot_row[pl.ds(s, 1), :] == iota, 1.0, 0.0).astype(jnp.bfloat16)
+                block = g_buf[c, rel // 8, rel // 4 % 2, rel // 2 % 2, rel % 2]
+                packed = jnp.dot(one_hot, block, preferred_element_type=jnp.float32)
+                pair[0, pl.ds(pl.multiple_of(s * cap, cap), cap), :] = packed.astype(jnp.bfloat16)
+
+    @jax.named_scope("pick")
+    def pick(e):
+        x_exp[e % 2] = jnp.dot(sel[e * per_expert:(e + 1) * per_expert, :], pair[0], preferred_element_type=jnp.float32).astype(jnp.bfloat16)
 
     @jax.named_scope("up_project")
-    def up_project(c, e0, e1):
-        @pl.loop(e0, e1)
-        def _(e):
-            i = c * experts + e
-            for copy in w13_copies(i):
-                copy.wait()
-            erows = pl.ds(pl.multiple_of(e * per_expert, per_expert), per_expert)
-            x_exp[...] = jnp.dot(sel[erows, :], pair[0], preferred_element_type=jnp.float32).astype(jnp.bfloat16)
-            for j in range(2):
-                for n in range(0, ff, CW):
-                    acc[j, erows, n:n + CW] += jnp.dot(x_exp[...], w13[i % 2, j, :, n:n + CW], preferred_element_type=jnp.float32)
-
-            @pl.when(i + 2 < chunks * experts)
-            def _():
-                for copy in w13_copies(i + 2):
-                    copy.start()
+    def up_project(c, e):
+        for copy in w13_copies(c, e):
+            copy.wait()
+        erows = slice(e * per_expert, (e + 1) * per_expert)
+        for j in range(2):
+            for n in range(0, ff, CW):
+                acc[j, erows, n:n + CW] += jnp.dot(x_exp[e % 2], w13[e % 2, j, :, n:n + CW], preferred_element_type=jnp.float32)
+        if e + 1 < experts:
+            pick(e + 1)
+        nc, ne = (c, e + 2) if e + 2 < experts else (c + 1, e + 2 - experts)
+
+        @pl.when(nc < chunks)
+        def _():
+            for copy in w13_copies(nc, ne):
+                copy.start()
 
     @jax.named_scope("build_pick")
     def build_pick():
@@ -197,13 +201,16 @@
 
         gather_core(k - 1).wait_recv()
         pack(k - 1)
-        up_project(k - 1, 0, experts // 2)
+        pick(0)
+        for e in range(experts // 2):
+            up_project(k - 1, e)
 
         @pl.when(k < chunks)
         def _():
             to_core(k)
 
-        up_project(k - 1, experts // 2, experts)
+        for e in range(experts // 2, experts):
+            up_project(k - 1, e)
 
     @pl.loop(0, chunks)
     def _(c):
@@ -269,40 +276,48 @@
 
     @jax.named_scope("down_project")
     def down_project(k):
-        @pl.loop(0, experts)
-        def _(e):
-            i = k * experts + e
-            w2_copy(i).wait()
-            erows = pl.ds(pl.multiple_of(e * per_expert, per_expert), per_expert)
-            o = jnp.dot(hid[erows, :], w2[i % 2], preferred_element_type=jnp.float32) * gate_col[erows, :]
+        for e in range(experts):
+            w2_copy(k, e).wait()
+            erows = slice(e * per_expert, (e + 1) * per_expert)
+            o = jnp.dot(hid[erows, :], w2[e % 2], preferred_element_type=jnp.float32) * gate_col[erows, :]
             hi = o.astype(jnp.bfloat16)
             pair[0, erows, :] = hi
             pair[1, erows, :] = (o - hi.astype(jnp.float32)).astype(jnp.bfloat16)
-
-            @pl.when(i + 2 < chunks * experts)
+            nk, ne = (k, e + 2) if e + 2 < experts else (k + 1, e + 2 - experts)
+
+            @pl.when(nk < chunks)
             def _():
-                w2_copy(i + 2).start()
+                w2_copy(nk, ne).start()
+
+    MT = 4 * cap
 
     @jax.named_scope("combine")
     def combine(k):
-        @pl.loop(0, sources // 2)
-        def _(m):
-            @pl.when((m == 1) & (k >= 1))
-            def _():
-                start_scatter(k - 1)
-
-            mrows = pl.ds(pl.multiple_of(m * 2 * cap, 2 * cap), 2 * cap)
-            pick = sel[mrows, :]
-            part = jnp.dot(pick, pair[0], preferred_element_type=jnp.float32)
-            part = part + jnp.dot(pick, pair[1], preferred_element_type=jnp.float32)
-            part = part.astype(jnp.bfloat16)
-            rz, ry, rx = xor(m // 4, zb), xor(m // 2 % 2, yb), xor(m % 2, xb)
-            for core in range(2):
-                s = m * 2 + core
-                slots = slot_col[pl.ds(pl.multiple_of(s * tok, tok), tok), :]
+        def gather_sum(m):
+            chosen = sel[m * MT:(m + 1) * MT, :]
+            total = jnp.dot(chosen, pair[0], preferred_element_type=jnp.float32)
+            total = total + jnp.dot(chosen, pair[1], preferred_element_type=jnp.float32)
+            part[m % 2] = total.astype(jnp.bfloat16)
+
+        def spread(m):
+            for u in range(MT // cap):
+                s = m * (MT // cap) + u
+                chip, core = s // 2, s % 2
+                slots = slot_col[s * tok:(s + 1) * tok, :]
                 place = jnp.where(slots == lax.broadcasted_iota(jnp.int32, (tok, cap), 1), 1.0, 0.0).astype(jnp.bfloat16)
-                spread = jnp.dot(place, part[core * cap:(core + 1) * cap, :], preferred_element_type=jnp.float32)
-                dense[k % 2, xor(core, cb), rz, ry, rx] = spread.astype(jnp.bfloat16)
+                block = jnp.dot(place, part[m % 2, u * cap:(u + 1) * cap, :], preferred_element_type=jnp.float32)
+                dense[k % 2, xor(core, cb), xor(chip // 4, zb), xor(chip // 2 % 2, yb), xor(chip % 2, xb)] = block.astype(jnp.bfloat16)
+
+        gather_sum(0)
+
+        @pl.when(k >= 1)
+        def _():
+            start_scatter(k - 1)
+
+        for m in range(1, rows // MT + 1):
+            if m < rows // MT:
+                gather_sum(m)
+            spread(m - 1)
 
     @pl.loop(0, chunks + 4)
     def _(k):
@@ -380,7 +395,8 @@
             pltpu.VMEM((2, 2, CW, ff), bf16),
             pltpu.VMEM((2, ff, CW), bf16),
             pltpu.VMEM((2, rows, CW), bf16),
-            pltpu.VMEM((rows // experts, CW), bf16),
+            pltpu.VMEM((2, rows // experts, CW), bf16),
+            pltpu.VMEM((2, rows // experts, CW), bf16),
             pltpu.VMEM((tok, hidden), bf16),
             pltpu.VMEM((rows, 1), f32),
             dma((chunks, 3, 3)), dma((chunks, 3, 3)), dma((chunks,)), dma((chunks,)), dma((chunks,)),

time: 253 us -> 215 us (0.85)
  Pallas kernels: 228 us -> 191 us
    pallas_call x1, Pallas kernels: 228 us -> 191 us  [moe_call(): pl.pallas_call(moe_kernel, out_shape=jax.ShapeDtypeStruct((tok, hidden),...]
where the time goes in v4:
time: 215 us
  Pallas kernels  191 us (89%)
  blocking collectives  10.9 us (5%)
  local copies, waits for them, and re-layouts  6.76 us (3%)
  other arithmetic  6.2 us (3%)
    pallas_call x1, Pallas kernels, moe_call(): pl.pallas_call(moe_kernel, out_shape=jax.ShapeDtypeStruct((tok, hidden),...  191 us
    all_to_all x1, blocking collectives, local_layer(): gates = lax.all_to_all(gate_send, ep_axes, 0, 0, tiled=True)  10.9 us
    unnamed x8, local copies, waits for them, and re-layouts  4.34 us

profile of v4, /device:TPU:0, one launch (start us, length us, event | category | flops | bytes accessed | tf_op | source)
XLA Modules:
  0.0 214.7 jit_solution(8383778670472464669)
XLA Ops:
  0.0 0.8 select_reduce_fusion.1
  0.8 10.9 %all_to_all.5 = f32[16,4,256]{2,1,0:T(4,128)S(1)} all-to-all(f32[16,4,256]{2,1,0:T(4,128)S(1)} %bitcast.40), channel_id=1, replica_groups=mesh['ez'=2,'ey'=2,'ex'=4] {'ez','ey','ex'}, dimensions={0} | all-to-all | bytes 131072 | tf_op jit(solution)/shard_map/all_to_all | solution.py:424
  11.7 0.1 compare_reduce_fusion
  11.8 0.6 reduce-window.14
  12.4 0.2 slice_reduce_fusion.1
  12.6 0.1 bitcast_select_fusion.2.slot_row
  12.7 0.0 copy-start.1
  12.7 0.1 add_add_fusion
  12.8 0.5 copy-done.1
  13.3 0.3 iota_compare_fusion
  13.6 1.3 select_reduce_fusion
  14.9 0.8 copy.39
  15.8 1.2 reduce-window.16
  16.9 0.2 slice_reduce_fusion
  17.2 0.2 reduce-window.19
  17.4 0.1 add_bitcast_fusion
  17.4 0.6 copy.50
  18.1 0.0 copy-start
  18.1 1.3 copy.35.rank_col
  19.4 0.0 copy-done
  19.5 0.6 copy.33
  20.1 1.6 bitcast_select_fusion.slot_col
  21.7 190.7 %shard_map.64 = bf16[256,2048]{1,0:T(8,128)(2,1)} custom-call(bf16[256,2048]{1,0:T(8,128)(2,1)} %x_hbm.1, s32[16,256]{1,0:T(8,128)} %copy-done.1, s32[4096,1]{1,0:T(8,128)} %bitcast_select_fusion.slot_col, s32[4,2048]{1,0:T(4,128)} %copy-done, s32[2048,4]{1,0:T(8,128)} %copy.35.rank_col, f32[4,2048]{1,0:T(4,128)} %bitcast.41, bf16[4,2048,1024]{2,1,0:T(8,128)(2,1)} %w1_hbm.1, ...), custom_call_target="tpu_custom_call" | custom-call | tf_op jit(solution)/shard_map/pallas_call | solution.py:384
  212.4 2.3 %copy.53 = bf16[256,2048]{1,0:T(8,128)(2,1)} copy(bf16[256,2048]{1,0:T(8,128)(2,1)} %shard_map.64) | data formatting | bytes 2097152
  (9 shorter events, 0.1 us)
Async XLA Ops:
  12.7 0.6 copy-start.1
  18.1 1.4 copy-start
